TPU v7x, 256 devices: a whole 4x4x8 slice. The times are simulated.
256 devices in a mesh: ctx: 64 (over z, x_hi, y), tp: 4 (over x_lo, core).
Axes of the slice: x: 4 (x_hi: 2, x_lo: 2; x = x_hi * 2 + x_lo), y: 4, z: 8, core: 2. Of those that a mesh axis runs over, the one named last changes fastest.
Arguments:
- queries: bfloat16 [32768, 4096], P('ctx', 'tp'), may hold values from -22 to 22
- keys: bfloat16 [32768, 512], P('ctx', 'tp'), may hold values from -22 to 22
- values: bfloat16 [32768, 512], P('ctx', 'tp'), may hold values from -36 to 36
- positions: int32 [3, 32768], P(None, 'ctx'), may hold values from 0 to 32767
- segment_ids: int32 [32768], replicated, may hold values from 0 to 31, never falling along the last dimension, each value on 1 to 2048 neighbouring positions
- out_weight: bfloat16 [4096, 8192], P('tp', 'ctx'), may hold values from -0.09375 to 0.09375
- residual: bfloat16 [32768, 8192], P(('ctx', 'tp')), may hold values from -3 to 3
Outputs:
- layer_out: bfloat16 [32768, 8192], P(('ctx', 'tp'))
Inputs may be any that keep to these rules, and one draw needn't show every extreme that they name: `segment_ids`: ids never fall along the sequence; each document has 1 to 2048 tokens, and one has exactly 2048.
All inputs are finite; a program needn't handle non-finite values.
Results may differ from a plain program's by a relative error of at most 0.013.
Values may be sent and summed in bfloat16 or wider, within the bound.
No kernel may reach another device: no remote copies, remote signals or barrier semaphores. Data moves between devices by JAX's collectives and lax.ppermute only.
A program may use at most 128 MiB of HBM per device.

v0:
```python
import functools
import math

import jax
import jax.numpy as jnp
from jax import lax
from jax.experimental import pallas as pl
from jax.experimental.pallas import tpu as pltpu
from jax.sharding import Mesh, PartitionSpec as P


HD = 128
theta_base = 1000000.0

CTX = ("z", "xh", "y")
TP = ("xl", "c")
XRING = ("xh", "xl")

TOK = 512
HEADS = 8
PIECE = 64
CHUNKS = 2
TQ = TOK // CHUNKS
BACK = 4
NEG = -1e30
EXP2_SCALE = math.log2(math.e) / math.sqrt(HD)


def from_behind(block, distance):
    size = math.prod(lax.axis_size(a) for a in CTX)
    route = [(i - distance, i) for i in range(distance, size)]
    return lax.ppermute(block, CTX, route)


def rotary_tables(positions):
    half_dim = HD // 2
    freq_index = jnp.arange(half_dim)
    inv_freq = theta_base ** (-2.0 * freq_index.astype(jnp.float32) / HD)
    first_end = HD // 8
    second_end = first_end + 3 * HD // 16
    place = positions.astype(jnp.float32)
    chosen = jnp.where(
        freq_index[None, :] < first_end,
        place[0][:, None],
        jnp.where(freq_index[None, :] < second_end, place[1][:, None], place[2][:, None]),
    )
    angle = chosen * inv_freq[None, :]
    cosine, sine = jnp.cos(angle), jnp.sin(angle)
    return jnp.concatenate([cosine, cosine], 1), jnp.concatenate([-sine, sine], 1)


def dot_nt(a, b):
    return lax.dot_general(a, b, (((1,), (1,)), ((), ())), preferred_element_type=jnp.float32)


def values_and_ones(value):
    return jnp.concatenate([value, jnp.ones_like(value)], axis=1)


def first_step(h, key, val, bias, rq_ref, m_ref, acc_ref):
    score = dot_nt(rq_ref[h], key) + bias
    peak = jnp.max(score, axis=1, keepdims=True)
    prob = jnp.exp2((score - peak) * EXP2_SCALE)
    m_ref[h] = jnp.broadcast_to(peak, (score.shape[0], HD))
    acc_ref[h] = jnp.dot(prob.astype(jnp.bfloat16), val, preferred_element_type=jnp.float32)


def next_step(h, key, val, bias, rq_ref, m_ref, acc_ref):
    score = dot_nt(rq_ref[h], key) + bias
    old = m_ref[h]
    new = jnp.maximum(old, jnp.broadcast_to(jnp.max(score, axis=1, keepdims=True), old.shape))
    keep = jnp.exp2((old - new) * EXP2_SCALE)
    wide = jnp.concatenate([new] * (score.shape[1] // HD), axis=1)
    prob = jnp.exp2((score - wide) * EXP2_SCALE)
    m_ref[h] = new
    acc_ref[h] = acc_ref[h] * jnp.concatenate([keep, keep], axis=1) + jnp.dot(
        prob.astype(jnp.bfloat16), val, preferred_element_type=jnp.float32
    )


def chunk_rows(i):
    return [pl.ds(b * 2 * PIECE + i * PIECE, PIECE) for b in range(TOK // (2 * PIECE))]


SMEM = pl.BlockSpec(memory_space=pltpu.SMEM)


def whole(shape):
    return pl.BlockSpec(shape, lambda n: (0,) * len(shape))


def attend_kernel(i, seg_s, qseg_ref, kseg_ref, q_ref, cos_ref, sin_ref, kv0, kv1, kv2, kv3, kv4, out_ref, rq_ref, m_ref, acc_ref):
    rows = chunk_rows(i)
    cosine = jnp.concatenate([cos_ref[r, :] for r in rows], axis=0)
    sine = jnp.concatenate([sin_ref[r, :] for r in rows], axis=0)
    for h in range(HEADS):
        x = jnp.concatenate([q_ref[r, h * HD : (h + 1) * HD] for r in rows], axis=0)
        x = x.astype(jnp.float32)
        rq_ref[h] = (x * cosine + pltpu.roll(x, HD // 2, 1) * sine).astype(jnp.bfloat16)
    qseg = jnp.concatenate([qseg_ref[r, :] for r in rows], axis=0)
    qseg = jnp.concatenate([qseg] * (TOK // HD), axis=1)
    row = lax.broadcasted_iota(jnp.int32, (TQ, TOK), 0)
    col = lax.broadcasted_iota(jnp.int32, (TQ, TOK), 1)
    token = (row // PIECE) * (2 * PIECE) + i * PIECE + row % PIECE
    bias = jnp.where((qseg == kseg_ref[BACK : BACK + 1, :]) & (col <= token), 0.0, NEG)
    for h in range(HEADS):
        first_step(h, kv0[:, :HD], values_and_ones(kv0[:, HD:]), bias, rq_ref, m_ref, acc_ref)
    for b, kv in enumerate((kv4, kv3, kv2, kv1)):

        @pl.when(seg_s[b * TOK + TOK - 1] == seg_s[BACK * TOK + i * PIECE])
        def _():
            bias = jnp.where(qseg == kseg_ref[b : b + 1, :], 0.0, NEG)
            for h in range(HEADS):
                next_step(h, kv[:, :HD], values_and_ones(kv[:, HD:]), bias, rq_ref, m_ref, acc_ref)

    for h in range(HEADS):
        full = acc_ref[h]
        out_ref[:, h * HD : (h + 1) * HD] = (full[:, :HD] / full[:, HD:]).astype(jnp.bfloat16)


def attend(i, seg, *blocks):
    return pl.pallas_call(
        functools.partial(attend_kernel, i),
        out_shape=jax.ShapeDtypeStruct((TQ, HEADS * HD), jnp.bfloat16),
        grid=(1,),
        in_specs=[SMEM] + [whole(b.shape) for b in blocks],
        out_specs=whole((TQ, HEADS * HD)),
        scratch_shapes=[
            pltpu.VMEM((HEADS, TQ, HD), jnp.bfloat16),
            pltpu.VMEM((HEADS, TQ, HD), jnp.float32),
            pltpu.VMEM((HEADS, TQ, 2 * HD), jnp.float32),
        ],
        compiler_params=pltpu.CompilerParams(vmem_limit_bytes=24 << 20),
    )(seg, *blocks)


def project_kernel(at, own_ref, oth_ref, w_ref, out_ref):
    n = pl.program_id(0)

    def total(core_bit):
        acc = None
        for j in range(4):
            a = (own_ref, oth_ref)[(j & 1) ^ core_bit][(j >> 1) ^ at[1]]
            w = jnp.concatenate([w_ref[0, at[3] ^ j], w_ref[1, at[3] ^ j]], axis=1)
            part = jnp.dot(a, w, preferred_element_type=jnp.float32)
            acc = part if acc is None else acc + part
        cols = pl.ds(pl.multiple_of(n * 2 * HD, 2 * HD), 2 * HD)
        for e in range(2):
            for i in range(CHUNKS):
                first = (e * CHUNKS + i) * TQ
                block = acc[first : first + TQ].astype(jnp.bfloat16)
                s = at[0] if e == 0 else 1 - at[0]
                out_ref[s, :, i, :, cols] = block.reshape(TQ // PIECE, PIECE, 2 * HD)

    for bit in range(2):

        @pl.when(at[2] == bit)
        def _():
            total(bit)


def project(at, own, oth, weight):
    steps = weight.shape[0] // 2
    out = (2, TQ // PIECE, CHUNKS, PIECE, 2 * steps * HD)
    return pl.pallas_call(
        project_kernel,
        out_shape=jax.ShapeDtypeStruct(out, jnp.bfloat16),
        grid=(steps,),
        in_specs=[SMEM]
        + [pl.BlockSpec(memory_space=pltpu.VMEM)] * 2
        + [pl.BlockSpec((2,) + weight.shape[1:], lambda n: (n, 0, 0, 0))],
        out_specs=whole(out),
        compiler_params=pltpu.CompilerParams(vmem_limit_bytes=36 << 20),
        name="project",
    )(at, own, oth, weight)


def finish_kernel(got_ref, res_ref, out_ref):
    srcs, zs = got_ref.shape[0], got_ref.shape[2] // HD
    for z in range(zs):
        for s in range(srcs):
            cols = pl.ds((z * srcs + s) * HD, HD)
            out_ref[:, cols] = (
                got_ref[s, :, z * HD : (z + 1) * HD].astype(jnp.float32)
                + res_ref[:, cols].astype(jnp.float32)
            ).astype(jnp.bfloat16)


def finish(got, residual):
    srcs, rows, cols = got.shape
    step = 32
    wide = pl.BlockSpec((step, srcs * cols), lambda r: (r, 0))
    return pl.pallas_call(
        finish_kernel,
        out_shape=jax.ShapeDtypeStruct(residual.shape, jnp.bfloat16),
        grid=(rows // step,),
        in_specs=[pl.BlockSpec((srcs, step, cols), lambda r: (0, r, 0)), wide],
        out_specs=wide,
        compiler_params=pltpu.CompilerParams(vmem_limit_bytes=16 << 20),
        name="finish",
    )(got, residual)


def swap4(block, axes, j):
    return lax.ppermute(block, axes, [(r, r ^ j) for r in range(4)])


def gather4(i, block, axes):
    j1 = swap4(block, axes, 1)
    j3 = swap4(block, axes, 3)
    j2 = swap4(*((j3, axes, 1) if i == 0 else (j1, axes, 3)))
    return block, j1, j2, j3


def other_core(block):
    return lax.ppermute(block, "c", [(0, 1), (1, 0)])


def on_device(queries, keys, values, positions, segment_ids, out_weight, residual):
    swap = [(y * 4 + t, t * 4 + y) for y in range(4) for t in range(4)]
    mine = lax.ppermute(out_weight, ("y",) + TP, swap)
    weight = lax.all_gather(mine, ("z", "y"), axis=0).reshape((8, 4) + mine.shape)

    cosine, sine = rotary_tables(positions)
    k32 = keys.astype(jnp.float32)
    flipped = jnp.concatenate([k32[:, HD // 2 :], k32[:, : HD // 2]], axis=1)
    rot_k = (k32 * cosine + flipped * sine).astype(jnp.bfloat16)
    kv = jnp.concatenate([rot_k, values], axis=1)
    behind = [from_behind(kv, d) for d in range(1, BACK + 1)]

    my_start = lax.axis_index(CTX) * TOK
    padded = jnp.concatenate([jnp.full((BACK * TOK,), -1, jnp.int32), segment_ids])
    seg = lax.dynamic_slice_in_dim(padded, my_start, (BACK + 1) * TOK, 0)
    qseg = jnp.broadcast_to(seg[BACK * TOK :, None], (TOK, HD))
    kseg = jnp.pad(seg.reshape(BACK + 1, TOK), ((0, 3), (0, 0)))

    near, far = [[], []], [[], []]
    for i in range(CHUNKS):
        own = attend(i, seg, qseg, kseg, queries, cosine, sine, kv, *behind)
        own, j1, j2, j3 = gather4(i, own, XRING)
        for side, blocks in ((near, (own, j2)), (far, (j1, j3))):
            for rows, block in zip(side, blocks):
                rows.append(block)
    own = jnp.concatenate([b for side in (near, far) for rows in side for b in rows], axis=0)
    own = own.reshape(2, 2 * TOK, HEADS * HD)
    oth = other_core(own)

    xh, xl, c, y = (lax.axis_index(a).astype(jnp.int32) for a in ("xh", "xl", "c", "y"))
    at = jnp.stack([xh, (y >> 1) ^ xl, (y & 1) ^ c, y])
    out = project(at, own, oth, weight)
    out = out.reshape(8, CHUNKS * PIECE, out.shape[-1])
    got = lax.all_to_all(out, XRING + ("c",), 0, 0)
    return finish(got, residual)


def solution(mesh):
    fine = Mesh(mesh.devices.reshape(8, 2, 4, 2, 2), CTX + TP)
    return jax.shard_map(
        on_device,
        mesh=fine,
        in_specs=(P(CTX, TP), P(CTX, TP), P(CTX, TP), P(None, CTX), P(), P(TP, CTX), P(CTX + TP, None)),
        out_specs=P(CTX + TP, None),
        check_vma=False,
    )
```

profile of v0, /device:TPU:1, one launch (start us, length us, event | category | flops | bytes accessed | tf_op | source)
XLA Modules:
  0.0 184.8 jit_solution(13627561204185088156)
XLA Ops:
  6.5 4.7 %collective-permute-start.11 = (bf16[1024,128]{1,0:T(8,128)(2,1)}, bf16[1024,128]{1,0:T(8,128)(2,1)S(1)}, u32[]{:S(2)}, u32[]{:S(2)}) collective-permute-start(bf16[1024,128]{1,0:T(8,128)(2,1)} %param.12), channel_id=1, source_target_pairs={{0,0},{1,4},{2,8},{3,12},{4,1},{5,5},{6,9},{7,13},{8,2},{9,6},{10,... | collective-permute-start | bytes 786440 | tf_op jit(solution)/shard_map/ppermute | solution.py:221
  11.3 5.0 %collective-permute-done.11 = bf16[1024,128]{1,0:T(8,128)(2,1)S(1)} collective-permute-done((bf16[1024,128]{1,0:T(8,128)(2,1)}, bf16[1024,128]{1,0:T(8,128)(2,1)S(1)}, u32[]{:S(2)}, u32[]{:S(2)}) %collective-permute-start.11) | collective-permute-done | bytes 262176 | tf_op jit(solution)/shard_map/ppermute | solution.py:221
  17.7 1.1 fusion.5
  18.8 1.7 fusion.4
  20.5 1.2 fusion.1
  21.8 1.3 collective-permute-start
  23.1 10.3 %collective-permute-start.1 = (bf16[512,256]{1,0:T(8,128)(2,1)S(1)}, bf16[512,256]{1,0:T(8,128)(2,1)S(1)}, u32[]{:S(2)}, u32[]{:S(2)}) collective-permute-start(bf16[512,256]{1,0:T(8,128)(2,1)S(1)} %pad_maximum_fusion.2.kv0), channel_id=1, source_target_pairs={{0,8},{4,12},{8,16},{12,20},{16,24},{20,28},{24,32},{28,36},{32,40... | collective-permute-start | bytes 786440 | tf_op jit(solution)/shard_map/ppermute | solution.py:32
  33.4 4.5 %collective-permute-start.2 = (bf16[512,256]{1,0:T(8,128)(2,1)S(1)}, bf16[512,256]{1,0:T(8,128)(2,1)S(1)}, u32[]{:S(2)}, u32[]{:S(2)}) collective-permute-start(bf16[512,256]{1,0:T(8,128)(2,1)S(1)} %pad_maximum_fusion.2.kv0), channel_id=1, source_target_pairs={{0,12},{4,16},{8,20},{12,24},{16,28},{20,32},{24,36},{28,40},{32,4... | collective-permute-start | bytes 786440 | tf_op jit(solution)/shard_map/ppermute | solution.py:32
  37.9 3.5 %collective-permute-start.3 = (bf16[512,256]{1,0:T(8,128)(2,1)S(1)}, bf16[512,256]{1,0:T(8,128)(2,1)S(1)}, u32[]{:S(2)}, u32[]{:S(2)}) collective-permute-start(bf16[512,256]{1,0:T(8,128)(2,1)S(1)} %pad_maximum_fusion.2.kv0), channel_id=1, source_target_pairs={{0,16},{4,20},{8,24},{12,28},{16,32},{20,36},{24,40},{28,44},{32,4... | collective-permute-start | bytes 786440 | tf_op jit(solution)/shard_map/ppermute | solution.py:32
  41.7 4.2 %collective-permute-done.2.kv3 = bf16[512,256]{1,0:T(8,128)(2,1)S(1)} collective-permute-done((bf16[512,256]{1,0:T(8,128)(2,1)S(1)}, bf16[512,256]{1,0:T(8,128)(2,1)S(1)}, u32[]{:S(2)}, u32[]{:S(2)}) %collective-permute-start.2) | collective-permute-done | bytes 262176 | tf_op jit(solution)/shard_map/ppermute | solution.py:32
  45.9 2.7 %shard_map.73 = bf16[256,1024]{1,0:T(8,128)(2,1)S(1)} custom-call(s32[2560]{0:T(1024)S(1)} %pad_dynamic-slice_fusion.1.seg_s, s32[512,128]{1,0:T(8,128)S(1)} %broadcast_in_dim.56.qseg_ref, s32[8,512]{1,0:T(8,128)S(1)} %pad.5.kseg_ref, bf16[512,1024]{1,0:T(8,128)(2,1)S(1)} %copy-done, f32[512,128]{1,0:T(8,128)S(1)} %get-tuple-element.7.cos_ref, ...), custom_call_target="tpu_custom_call" | custom-call | tf_op jit(solution)/shard_map/pallas_call | solution.py:122
  48.7 8.6 %collective-permute-start.4 = (bf16[256,1024]{1,0:T(8,128)(2,1)S(1)}, bf16[256,1024]{1,0:T(8,128)(2,1)S(1)}, u32[]{:S(2)}, u32[]{:S(2)}) collective-permute-start(bf16[256,1024]{1,0:T(8,128)(2,1)S(1)} %shard_map.73), channel_id=1, source_target_pairs={{0,18},{2,16},{16,2},{18,0},{1,19},{3,17},{17,3},{19,1},{4,22},{6,... | collective-permute-start | bytes 1572872 | tf_op jit(solution)/shard_map/ppermute | solution.py:205
  57.3 2.7 %shard_map.74 = bf16[256,1024]{1,0:T(8,128)(2,1)S(1)} custom-call(s32[2560]{0:T(1024)S(1)} %pad_dynamic-slice_fusion.1.seg_s, s32[512,128]{1,0:T(8,128)S(1)} %broadcast_in_dim.56.qseg_ref, s32[8,512]{1,0:T(8,128)S(1)} %pad.5.kseg_ref, bf16[512,1024]{1,0:T(8,128)(2,1)S(1)} %copy-done, f32[512,128]{1,0:T(8,128)S(1)} %get-tuple-element.7.cos_ref, ...), custom_call_target="tpu_custom_call" | custom-call | tf_op jit(solution)/shard_map/pallas_call | solution.py:122
  60.1 7.3 %collective-permute-done.4 = bf16[256,1024]{1,0:T(8,128)(2,1)S(1)} collective-permute-done((bf16[256,1024]{1,0:T(8,128)(2,1)S(1)}, bf16[256,1024]{1,0:T(8,128)(2,1)S(1)}, u32[]{:S(2)}, u32[]{:S(2)}) %collective-permute-start.4) | collective-permute-done | bytes 524320 | tf_op jit(solution)/shard_map/ppermute | solution.py:205
  67.4 3.7 %collective-permute-done.6 = bf16[256,1024]{1,0:T(8,128)(2,1)S(1)} collective-permute-done((bf16[256,1024]{1,0:T(8,128)(2,1)S(1)}, bf16[256,1024]{1,0:T(8,128)(2,1)S(1)}, u32[]{:S(2)}, u32[]{:S(2)}) %collective-permute-start.6) | collective-permute-done | bytes 524320 | tf_op jit(solution)/shard_map/ppermute | solution.py:205
  71.1 5.3 %collective-permute-start.7 = (bf16[256,1024]{1,0:T(8,128)(2,1)S(1)}, bf16[256,1024]{1,0:T(8,128)(2,1)S(1)}, u32[]{:S(2)}, u32[]{:S(2)}) collective-permute-start(bf16[256,1024]{1,0:T(8,128)(2,1)S(1)} %collective-permute-done.6), channel_id=1, source_target_pairs={{0,18},{2,16},{16,2},{18,0},{1,19},{3,17},{17,3},{19,1},{4,22},{6,... | collective-permute-start | bytes 1572872 | tf_op jit(solution)/shard_map/ppermute | solution.py:205
  76.4 0.9 constant_dynamic-update-slice_fusion.7
  77.3 0.8 constant_dynamic-update-slice_fusion.6
  78.1 4.2 %collective-permute-done.5 = bf16[256,1024]{1,0:T(8,128)(2,1)S(1)} collective-permute-done((bf16[256,1024]{1,0:T(8,128)(2,1)S(1)}, bf16[256,1024]{1,0:T(8,128)(2,1)S(1)}, u32[]{:S(2)}, u32[]{:S(2)}) %collective-permute-start.5) | collective-permute-done | bytes 524320 | tf_op jit(solution)/shard_map/ppermute | solution.py:205
  82.3 0.8 constant_dynamic-update-slice_fusion.5
  83.2 0.9 constant_dynamic-update-slice_fusion.4
  84.0 9.6 %collective-permute-done.8 = bf16[256,1024]{1,0:T(8,128)(2,1)S(1)} collective-permute-done((bf16[256,1024]{1,0:T(8,128)(2,1)S(1)}, bf16[256,1024]{1,0:T(8,128)(2,1)S(1)}, u32[]{:S(2)}, u32[]{:S(2)}) %collective-permute-start.8) | collective-permute-done | bytes 524320 | tf_op jit(solution)/shard_map/ppermute | solution.py:205
  93.7 0.8 constant_dynamic-update-slice_fusion.3
  94.5 0.9 constant_dynamic-update-slice_fusion.2
  95.3 0.8 constant_dynamic-update-slice_fusion.1
  96.2 0.8 constant_dynamic-update-slice_fusion
  97.0 4.3 %collective-permute-start.10 = (bf16[2,1024,1024]{2,1,0:T(8,128)(2,1)}, bf16[2,1024,1024]{2,1,0:T(8,128)(2,1)}, u32[]{:S(2)}, u32[]{:S(2)}) collective-permute-start(bf16[2,1024,1024]{2,1,0:T(8,128)(2,1)} %bitcast.7.own_ref), channel_id=1, source_target_pairs={{0,1},{1,0},{2,3},{3,2},{4,5},{5,4},{6,7},{7,6},{8,9},{9,8},{10,11... | collective-permute-start | bytes 12582920 | tf_op jit(solution)/shard_map/ppermute | solution.py:216
  101.4 7.1 %collective-permute-done.10.oth_ref = bf16[2,1024,1024]{2,1,0:T(8,128)(2,1)} collective-permute-done((bf16[2,1024,1024]{2,1,0:T(8,128)(2,1)}, bf16[2,1024,1024]{2,1,0:T(8,128)(2,1)}, u32[]{:S(2)}, u32[]{:S(2)}) %collective-permute-start.10) | collective-permute-done | bytes 4194336 | tf_op jit(solution)/shard_map/ppermute | solution.py:216
  108.4 22.0 %all-gather.3.cloned.1.call-done = bf16[32768,128]{1,0:T(8,128)(2,1)} async-done(((bf16[1024,128]{1,0:T(8,128)(2,1)}), bf16[32768,128]{1,0:T(8,128)(2,1)}) %all-gather.3.cloned.1.call-update) | async-done | bytes 8388624 | tf_op jit(solution)/shard_map/all_gather | solution.py:222
  130.5 13.5 %project.1 = bf16[2,4,2,64,1024]{4,3,2,1,0:T(8,128)(2,1)S(1)} custom-call(s32[4]{0:T(128)S(1)} %pad_add_fusion.at, bf16[2,1024,1024]{2,1,0:T(8,128)(2,1)} %bitcast.7.own_ref, bf16[2,1024,1024]{2,1,0:T(8,128)(2,1)} %collective-permute-done.10.oth_ref, bf16[8,4,1024,128]{3,2,1,0:T(8,128)(2,1)} %bitcast.11), custom_call_target="tpu_custom_call" | custom-call | tf_op jit(solution)/shard_map/project/pallas_call | solution.py:165
  144.0 31.8 %all_to_all.5.got_ref = bf16[8,128,1024]{2,1,0:T(8,128)(2,1)S(1)} all-to-all(bf16[8,128,1024]{2,1,0:T(8,128)(2,1)S(1)} %bitcast.10), channel_id=1, replica_groups=mesh['z'=8,'xh'=2,'y'=4,'xl'=2,'c'=2] {'xh','xl','c'}, dimensions={0} | all-to-all | bytes 4194304 | tf_op jit(solution)/shard_map/all_to_all | solution.py:252
  175.8 2.2 %finish.1 = bf16[128,8192]{1,0:T(8,128)(2,1)} custom-call(bf16[8,128,1024]{2,1,0:T(8,128)(2,1)S(1)} %all_to_all.5.got_ref, bf16[128,8192]{1,0:T(8,128)(2,1)S(1)} %copy-done.1), custom_call_target="tpu_custom_call" | custom-call | tf_op jit(solution)/shard_map/finish/pallas_call | solution.py:193
  (32 shorter events, 2.0 us)
Async XLA Ops:
  6.5 15.2 %copy-start.4 = (bf16[512,128]{1,0:T(8,128)(2,1)S(1)}, bf16[512,128]{1,0:T(8,128)(2,1)}, u32[]{:S(2)}) copy-start(bf16[512,128]{1,0:T(8,128)(2,1)} %param.9) | copy-start | bytes 393220
  6.5 34.9 %copy-start.2 = (s32[32768]{0:T(1024)S(1)}, s32[32768]{0:T(1024)}, u32[]{:S(2)}) copy-start(s32[32768]{0:T(1024)} %param.11) | copy-start | bytes 393220
  6.5 39.4 %copy-start = (bf16[512,1024]{1,0:T(8,128)(2,1)S(1)}, bf16[512,1024]{1,0:T(8,128)(2,1)}, u32[]{:S(2)}) copy-start(bf16[512,1024]{1,0:T(8,128)(2,1)} %q_ref.3) | copy-start | bytes 3145732
  6.5 123.9 %all-gather.3.cloned.1.call-start = ((), (), s32[]{:S(2)}) async-start(), calls=%async_computation.1 | async-start | bytes 8650752 | tf_op jit(solution)/shard_map/all_gather | solution.py:222
  6.5 9.7 %collective-permute-start.11 = (bf16[1024,128]{1,0:T(8,128)(2,1)}, bf16[1024,128]{1,0:T(8,128)(2,1)S(1)}, u32[]{:S(2)}, u32[]{:S(2)}) collective-permute-start(bf16[1024,128]{1,0:T(8,128)(2,1)} %param.12), channel_id=1, source_target_pairs={{0,0},{1,4},{2,8},{3,12},{4,1},{5,5},{6,9},{7,13},{8,2},{9,6},{10,... | collective-permute-start | bytes 786440 | tf_op jit(solution)/shard_map/ppermute | solution.py:221
  16.3 0.7 copy-start.3
  21.8 19.9 %collective-permute-start = (bf16[512,256]{1,0:T(8,128)(2,1)S(1)}, bf16[512,256]{1,0:T(8,128)(2,1)S(1)}, u32[]{:S(2)}, u32[]{:S(2)}) collective-permute-start(bf16[512,256]{1,0:T(8,128)(2,1)S(1)} %pad_maximum_fusion.2.kv0), channel_id=1, source_target_pairs={{0,4},{4,8},{8,12},{12,16},{16,20},{20,24},{24,28},{28,32},{32,36}... | collective-permute-start | bytes 786440 | tf_op jit(solution)/shard_map/ppermute | solution.py:32
  23.1 18.6 %collective-permute-start.1 = (bf16[512,256]{1,0:T(8,128)(2,1)S(1)}, bf16[512,256]{1,0:T(8,128)(2,1)S(1)}, u32[]{:S(2)}, u32[]{:S(2)}) collective-permute-start(bf16[512,256]{1,0:T(8,128)(2,1)S(1)} %pad_maximum_fusion.2.kv0), channel_id=1, source_target_pairs={{0,8},{4,12},{8,16},{12,20},{16,24},{20,28},{24,32},{28,36},{32,40... | collective-permute-start | bytes 786440 | tf_op jit(solution)/shard_map/ppermute | solution.py:32
  33.4 12.4 %collective-permute-start.2 = (bf16[512,256]{1,0:T(8,128)(2,1)S(1)}, bf16[512,256]{1,0:T(8,128)(2,1)S(1)}, u32[]{:S(2)}, u32[]{:S(2)}) collective-permute-start(bf16[512,256]{1,0:T(8,128)(2,1)S(1)} %pad_maximum_fusion.2.kv0), channel_id=1, source_target_pairs={{0,12},{4,16},{8,20},{12,24},{16,28},{20,32},{24,36},{28,40},{32,4... | collective-permute-start | bytes 786440 | tf_op jit(solution)/shard_map/ppermute | solution.py:32
  37.9 7.9 %collective-permute-start.3 = (bf16[512,256]{1,0:T(8,128)(2,1)S(1)}, bf16[512,256]{1,0:T(8,128)(2,1)S(1)}, u32[]{:S(2)}, u32[]{:S(2)}) collective-permute-start(bf16[512,256]{1,0:T(8,128)(2,1)S(1)} %pad_maximum_fusion.2.kv0), channel_id=1, source_target_pairs={{0,16},{4,20},{8,24},{12,28},{16,32},{20,36},{24,40},{28,44},{32,4... | collective-permute-start | bytes 786440 | tf_op jit(solution)/shard_map/ppermute | solution.py:32
  48.7 18.7 %collective-permute-start.4 = (bf16[256,1024]{1,0:T(8,128)(2,1)S(1)}, bf16[256,1024]{1,0:T(8,128)(2,1)S(1)}, u32[]{:S(2)}, u32[]{:S(2)}) collective-permute-start(bf16[256,1024]{1,0:T(8,128)(2,1)S(1)} %shard_map.73), channel_id=1, source_target_pairs={{0,18},{2,16},{16,2},{18,0},{1,19},{3,17},{17,3},{19,1},{4,22},{6,... | collective-permute-start | bytes 1572872 | tf_op jit(solution)/shard_map/ppermute | solution.py:205
  60.0 11.1 %collective-permute-start.6 = (bf16[256,1024]{1,0:T(8,128)(2,1)S(1)}, bf16[256,1024]{1,0:T(8,128)(2,1)S(1)}, u32[]{:S(2)}, u32[]{:S(2)}) collective-permute-start(bf16[256,1024]{1,0:T(8,128)(2,1)S(1)} %shard_map.74), channel_id=1, source_target_pairs={{0,2},{2,0},{16,18},{18,16},{1,3},{3,1},{17,19},{19,17},{4,6},{6,4... | collective-permute-start | bytes 1572872 | tf_op jit(solution)/shard_map/ppermute | solution.py:205
  67.4 14.9 %collective-permute-start.5 = (bf16[256,1024]{1,0:T(8,128)(2,1)S(1)}, bf16[256,1024]{1,0:T(8,128)(2,1)S(1)}, u32[]{:S(2)}, u32[]{:S(2)}) collective-permute-start(bf16[256,1024]{1,0:T(8,128)(2,1)S(1)} %collective-permute-done.4), channel_id=1, source_target_pairs={{0,2},{2,0},{16,18},{18,16},{1,3},{3,1},{17,19},{19,17},{4,6},{6,4... | collective-permute-start | bytes 1572872 | tf_op jit(solution)/shard_map/ppermute | solution.py:205
  71.1 12.1 %collective-permute-start.7 = (bf16[256,1024]{1,0:T(8,128)(2,1)S(1)}, bf16[256,1024]{1,0:T(8,128)(2,1)S(1)}, u32[]{:S(2)}, u32[]{:S(2)}) collective-permute-start(bf16[256,1024]{1,0:T(8,128)(2,1)S(1)} %collective-permute-done.6), channel_id=1, source_target_pairs={{0,18},{2,16},{16,2},{18,0},{1,19},{3,17},{17,3},{19,1},{4,22},{6,... | collective-permute-start | bytes 1572872 | tf_op jit(solution)/shard_map/ppermute | solution.py:205
  76.4 17.3 %collective-permute-start.8 = (bf16[256,1024]{1,0:T(8,128)(2,1)S(1)}, bf16[256,1024]{1,0:T(8,128)(2,1)S(1)}, u32[]{:S(2)}, u32[]{:S(2)}) collective-permute-start(bf16[256,1024]{1,0:T(8,128)(2,1)S(1)} %shard_map.73), channel_id=1, source_target_pairs={{0,2},{2,0},{16,18},{18,16},{1,3},{3,1},{17,19},{19,17},{4,6},{6,4... | collective-permute-start | bytes 1572872 | tf_op jit(solution)/shard_map/ppermute | solution.py:205
  76.4 19.8 %collective-permute-start.9 = (bf16[256,1024]{1,0:T(8,128)(2,1)S(1)}, bf16[256,1024]{1,0:T(8,128)(2,1)S(1)}, u32[]{:S(2)}, u32[]{:S(2)}) collective-permute-start(bf16[256,1024]{1,0:T(8,128)(2,1)S(1)} %shard_map.74), channel_id=1, source_target_pairs={{0,18},{2,16},{16,2},{18,0},{1,19},{3,17},{17,3},{19,1},{4,22},{6,... | collective-permute-start | bytes 1572872 | tf_op jit(solution)/shard_map/ppermute | solution.py:205
  97.0 11.5 %collective-permute-start.10 = (bf16[2,1024,1024]{2,1,0:T(8,128)(2,1)}, bf16[2,1024,1024]{2,1,0:T(8,128)(2,1)}, u32[]{:S(2)}, u32[]{:S(2)}) collective-permute-start(bf16[2,1024,1024]{2,1,0:T(8,128)(2,1)} %bitcast.7.own_ref), channel_id=1, source_target_pairs={{0,1},{1,0},{2,3},{3,2},{4,5},{5,4},{6,7},{7,6},{8,9},{9,8},{10,11... | collective-permute-start | bytes 12582920 | tf_op jit(solution)/shard_map/ppermute | solution.py:216
  144.0 31.8 %copy-start.1 = (bf16[128,8192]{1,0:T(8,128)(2,1)S(1)}, bf16[128,8192]{1,0:T(8,128)(2,1)}, u32[]{:S(2)}) copy-start(bf16[128,8192]{1,0:T(8,128)(2,1)} %res_ref.1) | copy-start | bytes 6291460
Sparse Core Ops, SparseCore 0:
  17.1 113.3 all-gather.2
where the time goes:
time: 185 us
  waiting for transfers between devices  63.1 us (34%)
  starting transfers between devices  42.7 us (23%)
  blocking collectives  31.8 us (17%)
  Pallas kernels  21.1 us (11%)
  between operations  13.5 us (7%)
  local copies, waits for them, and re-layouts  8.84 us (5%)
  other arithmetic  3.71 us (2%)
    all_to_all x1, blocking collectives, on_device(): got = lax.all_to_all(out, XRING + ('c',), 0, 0)  31.8 us
    ppermute x6, waiting for transfers between devices, swap4(): return lax.ppermute(block, axes, [(r, r ^ j) for r in range(4)])  24.8 us
    all_gather x1, waiting for transfers between devices, on_device(): lax.all_gather(mine, ('z', 'y'), axis=0).reshape((8, 4) + mine.shape)  22 us
    ppermute x4, starting transfers between devices, from_behind(): return lax.ppermute(block, CTX, route)  19.6 us
    ppermute x6, starting transfers between devices, swap4(): return lax.ppermute(block, axes, [(r, r ^ j) for r in range(4)])  14 us
    pallas_call x1, Pallas kernels, project(): pl.pallas_call(project_kernel, out_shape=jax.ShapeDtypeStruct(out, jnp.bf...  13.5 us
    ppermute x1, waiting for transfers between devices, other_core(): return lax.ppermute(block, 'c', [(0, 1), (1, 0)])  7.05 us
    unnamed x17, local copies, waits for them, and re-layouts  6.61 us
  transfers between devices with their start and end apart: 13, of which 8 were waited for; matrix products, arithmetic and copies ran while one was open for 6% of the time, Pallas kernels for 3%

commit v1 on v0

--- a/solution.py
+++ b/solution.py
@@ -135,41 +135,31 @@
 
 
 def project_kernel(at, own_ref, oth_ref, w_ref, out_ref):
-    n = pl.program_id(0)
-
-    def total(core_bit):
-        acc = None
-        for j in range(4):
-            a = (own_ref, oth_ref)[(j & 1) ^ core_bit][(j >> 1) ^ at[1]]
-            w = jnp.concatenate([w_ref[0, at[3] ^ j], w_ref[1, at[3] ^ j]], axis=1)
-            part = jnp.dot(a, w, preferred_element_type=jnp.float32)
-            acc = part if acc is None else acc + part
-        cols = pl.ds(pl.multiple_of(n * 2 * HD, 2 * HD), 2 * HD)
-        for e in range(2):
-            for i in range(CHUNKS):
-                first = (e * CHUNKS + i) * TQ
-                block = acc[first : first + TQ].astype(jnp.bfloat16)
-                s = at[0] if e == 0 else 1 - at[0]
-                out_ref[s, :, i, :, cols] = block.reshape(TQ // PIECE, PIECE, 2 * HD)
-
-    for bit in range(2):
-
-        @pl.when(at[2] == bit)
-        def _():
-            total(bit)
+    places = [at[1] ^ (2 * far + core) for core in range(2) for far in range(2)]
+    w = jnp.concatenate(
+        [jnp.concatenate([w_ref[0, p], w_ref[1, p]], axis=1) for p in places], axis=0
+    )
+    a = jnp.concatenate([own_ref[0], own_ref[1], oth_ref[0], oth_ref[1]], axis=1)
+    acc = jnp.dot(a, w, preferred_element_type=jnp.float32)
+    for e in range(2):
+        for i in range(CHUNKS):
+            first = (e * CHUNKS + i) * TQ
+            block = acc[first : first + TQ].astype(jnp.bfloat16)
+            s = at[0] if e == 0 else 1 - at[0]
+            out_ref[s, :, i] = block.reshape(TQ // PIECE, PIECE, 2 * HD)
 
 
 def project(at, own, oth, weight):
     steps = weight.shape[0] // 2
-    out = (2, TQ // PIECE, CHUNKS, PIECE, 2 * steps * HD)
+    rows = (2, TQ // PIECE, CHUNKS, PIECE)
     return pl.pallas_call(
         project_kernel,
-        out_shape=jax.ShapeDtypeStruct(out, jnp.bfloat16),
+        out_shape=jax.ShapeDtypeStruct(rows + (2 * steps * HD,), jnp.bfloat16),
         grid=(steps,),
         in_specs=[SMEM]
         + [pl.BlockSpec(memory_space=pltpu.VMEM)] * 2
         + [pl.BlockSpec((2,) + weight.shape[1:], lambda n: (n, 0, 0, 0))],
-        out_specs=whole(out),
+        out_specs=pl.BlockSpec(rows + (2 * HD,), lambda n: (0, 0, 0, 0, n)),
         compiler_params=pltpu.CompilerParams(vmem_limit_bytes=36 << 20),
         name="project",
     )(at, own, oth, weight)
@@ -188,7 +178,7 @@
 
 def finish(got, residual):
     srcs, rows, cols = got.shape
-    step = 32
+    step = 64
     wide = pl.BlockSpec((step, srcs * cols), lambda r: (r, 0))
     return pl.pallas_call(
         finish_kernel,
@@ -245,8 +235,8 @@
     own = own.reshape(2, 2 * TOK, HEADS * HD)
     oth = other_core(own)
 
-    xh, xl, c, y = (lax.axis_index(a).astype(jnp.int32) for a in ("xh", "xl", "c", "y"))
-    at = jnp.stack([xh, (y >> 1) ^ xl, (y & 1) ^ c, y])
+    xh, xl, c = (lax.axis_index(a).astype(jnp.int32) for a in ("xh", "xl", "c"))
+    at = jnp.stack([xh, 2 * xl + c])
     out = project(at, own, oth, weight)
     out = out.reshape(8, CHUNKS * PIECE, out.shape[-1])
     got = lax.all_to_all(out, XRING + ("c",), 0, 0)

time: 185 us -> 185 us (level)
  no operation moved by 1% of the time
where the time goes in v1:
time: 185 us
  waiting for transfers between devices  63.1 us (34%)
  starting transfers between devices  42.7 us (23%)
  blocking collectives  31.8 us (17%)
  Pallas kernels  20.9 us (11%)
  between operations  13.5 us (7%)
  local copies, waits for them, and re-layouts  8.84 us (5%)
  other arithmetic  3.71 us (2%)
    all_to_all x1, blocking collectives, on_device(): got = lax.all_to_all(out, XRING + ('c',), 0, 0)  31.8 us
    ppermute x6, waiting for transfers between devices, swap4(): return lax.ppermute(block, axes, [(r, r ^ j) for r in range(4)])  24.8 us
    all_gather x1, waiting for transfers between devices, on_device(): lax.all_gather(mine, ('z', 'y'), axis=0).reshape((8, 4) + mine.shape)  22 us
    ppermute x4, starting transfers between devices, from_behind(): return lax.ppermute(block, CTX, route)  19.6 us
    ppermute x6, starting transfers between devices, swap4(): return lax.ppermute(block, axes, [(r, r ^ j) for r in range(4)])  14 us
    pallas_call x1, Pallas kernels, project(): pl.pallas_call(project_kernel, out_shape=jax.ShapeDtypeStruct(rows + (2 *...  13.7 us
    ppermute x1, waiting for transfers between devices, other_core(): return lax.ppermute(block, 'c', [(0, 1), (1, 0)])  7.05 us
    unnamed x17, local copies, waits for them, and re-layouts  6.61 us
  transfers between devices with their start and end apart: 13, of which 8 were waited for; matrix products, arithmetic and copies ran while one was open for 6% of the time, Pallas kernels for 3%

profile of v1, /device:TPU:1, one launch (start us, length us, event | category | flops | bytes accessed | tf_op | source)
XLA Modules:
  0.0 184.6 jit_solution(14412561444328153495)
XLA Ops:
  6.5 4.7 %collective-permute-start.11 = (bf16[1024,128]{1,0:T(8,128)(2,1)}, bf16[1024,128]{1,0:T(8,128)(2,1)S(1)}, u32[]{:S(2)}, u32[]{:S(2)}) collective-permute-start(bf16[1024,128]{1,0:T(8,128)(2,1)} %param.12), channel_id=1, source_target_pairs={{0,0},{1,4},{2,8},{3,12},{4,1},{5,5},{6,9},{7,13},{8,2},{9,6},{10,... | collective-permute-start | bytes 786440 | tf_op jit(solution)/shard_map/ppermute | solution.py:211
  11.3 5.0 %collective-permute-done.11 = bf16[1024,128]{1,0:T(8,128)(2,1)S(1)} collective-permute-done((bf16[1024,128]{1,0:T(8,128)(2,1)}, bf16[1024,128]{1,0:T(8,128)(2,1)S(1)}, u32[]{:S(2)}, u32[]{:S(2)}) %collective-permute-start.11) | collective-permute-done | bytes 262176 | tf_op jit(solution)/shard_map/ppermute | solution.py:211
  17.7 1.1 fusion.5
  18.8 1.7 fusion.4
  20.5 1.2 fusion.1
  21.8 1.3 collective-permute-start
  23.1 10.3 %collective-permute-start.1 = (bf16[512,256]{1,0:T(8,128)(2,1)S(1)}, bf16[512,256]{1,0:T(8,128)(2,1)S(1)}, u32[]{:S(2)}, u32[]{:S(2)}) collective-permute-start(bf16[512,256]{1,0:T(8,128)(2,1)S(1)} %pad_maximum_fusion.2.kv0), channel_id=1, source_target_pairs={{0,8},{4,12},{8,16},{12,20},{16,24},{20,28},{24,32},{28,36},{32,40... | collective-permute-start | bytes 786440 | tf_op jit(solution)/shard_map/ppermute | solution.py:32
  33.4 4.5 %collective-permute-start.2 = (bf16[512,256]{1,0:T(8,128)(2,1)S(1)}, bf16[512,256]{1,0:T(8,128)(2,1)S(1)}, u32[]{:S(2)}, u32[]{:S(2)}) collective-permute-start(bf16[512,256]{1,0:T(8,128)(2,1)S(1)} %pad_maximum_fusion.2.kv0), channel_id=1, source_target_pairs={{0,12},{4,16},{8,20},{12,24},{16,28},{20,32},{24,36},{28,40},{32,4... | collective-permute-start | bytes 786440 | tf_op jit(solution)/shard_map/ppermute | solution.py:32
  37.9 3.5 %collective-permute-start.3 = (bf16[512,256]{1,0:T(8,128)(2,1)S(1)}, bf16[512,256]{1,0:T(8,128)(2,1)S(1)}, u32[]{:S(2)}, u32[]{:S(2)}) collective-permute-start(bf16[512,256]{1,0:T(8,128)(2,1)S(1)} %pad_maximum_fusion.2.kv0), channel_id=1, source_target_pairs={{0,16},{4,20},{8,24},{12,28},{16,32},{20,36},{24,40},{28,44},{32,4... | collective-permute-start | bytes 786440 | tf_op jit(solution)/shard_map/ppermute | solution.py:32
  41.7 4.2 %collective-permute-done.2.kv3 = bf16[512,256]{1,0:T(8,128)(2,1)S(1)} collective-permute-done((bf16[512,256]{1,0:T(8,128)(2,1)S(1)}, bf16[512,256]{1,0:T(8,128)(2,1)S(1)}, u32[]{:S(2)}, u32[]{:S(2)}) %collective-permute-start.2) | collective-permute-done | bytes 262176 | tf_op jit(solution)/shard_map/ppermute | solution.py:32
  45.9 2.7 %shard_map.73 = bf16[256,1024]{1,0:T(8,128)(2,1)S(1)} custom-call(s32[2560]{0:T(1024)S(1)} %pad_dynamic-slice_fusion.1.seg_s, s32[512,128]{1,0:T(8,128)S(1)} %broadcast_in_dim.56.qseg_ref, s32[8,512]{1,0:T(8,128)S(1)} %pad.5.kseg_ref, bf16[512,1024]{1,0:T(8,128)(2,1)S(1)} %copy-done, f32[512,128]{1,0:T(8,128)S(1)} %get-tuple-element.7.cos_ref, ...), custom_call_target="tpu_custom_call" | custom-call | tf_op jit(solution)/shard_map/pallas_call | solution.py:122
  48.7 8.6 %collective-permute-start.4 = (bf16[256,1024]{1,0:T(8,128)(2,1)S(1)}, bf16[256,1024]{1,0:T(8,128)(2,1)S(1)}, u32[]{:S(2)}, u32[]{:S(2)}) collective-permute-start(bf16[256,1024]{1,0:T(8,128)(2,1)S(1)} %shard_map.73), channel_id=1, source_target_pairs={{0,18},{2,16},{16,2},{18,0},{1,19},{3,17},{17,3},{19,1},{4,22},{6,... | collective-permute-start | bytes 1572872 | tf_op jit(solution)/shard_map/ppermute | solution.py:195
  57.3 2.7 %shard_map.74 = bf16[256,1024]{1,0:T(8,128)(2,1)S(1)} custom-call(s32[2560]{0:T(1024)S(1)} %pad_dynamic-slice_fusion.1.seg_s, s32[512,128]{1,0:T(8,128)S(1)} %broadcast_in_dim.56.qseg_ref, s32[8,512]{1,0:T(8,128)S(1)} %pad.5.kseg_ref, bf16[512,1024]{1,0:T(8,128)(2,1)S(1)} %copy-done, f32[512,128]{1,0:T(8,128)S(1)} %get-tuple-element.7.cos_ref, ...), custom_call_target="tpu_custom_call" | custom-call | tf_op jit(solution)/shard_map/pallas_call | solution.py:122
  60.1 7.3 %collective-permute-done.4 = bf16[256,1024]{1,0:T(8,128)(2,1)S(1)} collective-permute-done((bf16[256,1024]{1,0:T(8,128)(2,1)S(1)}, bf16[256,1024]{1,0:T(8,128)(2,1)S(1)}, u32[]{:S(2)}, u32[]{:S(2)}) %collective-permute-start.4) | collective-permute-done | bytes 524320 | tf_op jit(solution)/shard_map/ppermute | solution.py:195
  67.4 3.7 %collective-permute-done.6 = bf16[256,1024]{1,0:T(8,128)(2,1)S(1)} collective-permute-done((bf16[256,1024]{1,0:T(8,128)(2,1)S(1)}, bf16[256,1024]{1,0:T(8,128)(2,1)S(1)}, u32[]{:S(2)}, u32[]{:S(2)}) %collective-permute-start.6) | collective-permute-done | bytes 524320 | tf_op jit(solution)/shard_map/ppermute | solution.py:195
  71.1 5.3 %collective-permute-start.7 = (bf16[256,1024]{1,0:T(8,128)(2,1)S(1)}, bf16[256,1024]{1,0:T(8,128)(2,1)S(1)}, u32[]{:S(2)}, u32[]{:S(2)}) collective-permute-start(bf16[256,1024]{1,0:T(8,128)(2,1)S(1)} %collective-permute-done.6), channel_id=1, source_target_pairs={{0,18},{2,16},{16,2},{18,0},{1,19},{3,17},{17,3},{19,1},{4,22},{6,... | collective-permute-start | bytes 1572872 | tf_op jit(solution)/shard_map/ppermute | solution.py:195
  76.4 0.9 constant_dynamic-update-slice_fusion.7
  77.3 0.8 constant_dynamic-update-slice_fusion.6
  78.1 4.2 %collective-permute-done.5 = bf16[256,1024]{1,0:T(8,128)(2,1)S(1)} collective-permute-done((bf16[256,1024]{1,0:T(8,128)(2,1)S(1)}, bf16[256,1024]{1,0:T(8,128)(2,1)S(1)}, u32[]{:S(2)}, u32[]{:S(2)}) %collective-permute-start.5) | collective-permute-done | bytes 524320 | tf_op jit(solution)/shard_map/ppermute | solution.py:195
  82.3 0.8 constant_dynamic-update-slice_fusion.5
  83.2 0.9 constant_dynamic-update-slice_fusion.4
  84.0 9.6 %collective-permute-done.8 = bf16[256,1024]{1,0:T(8,128)(2,1)S(1)} collective-permute-done((bf16[256,1024]{1,0:T(8,128)(2,1)S(1)}, bf16[256,1024]{1,0:T(8,128)(2,1)S(1)}, u32[]{:S(2)}, u32[]{:S(2)}) %collective-permute-start.8) | collective-permute-done | bytes 524320 | tf_op jit(solution)/shard_map/ppermute | solution.py:195
  93.7 0.8 constant_dynamic-update-slice_fusion.3
  94.5 0.9 constant_dynamic-update-slice_fusion.2
  95.3 0.8 constant_dynamic-update-slice_fusion.1
  96.2 0.8 constant_dynamic-update-slice_fusion
  97.0 4.3 %collective-permute-start.10 = (bf16[2,1024,1024]{2,1,0:T(8,128)(2,1)}, bf16[2,1024,1024]{2,1,0:T(8,128)(2,1)}, u32[]{:S(2)}, u32[]{:S(2)}) collective-permute-start(bf16[2,1024,1024]{2,1,0:T(8,128)(2,1)} %bitcast.5.own_ref), channel_id=1, source_target_pairs={{0,1},{1,0},{2,3},{3,2},{4,5},{5,4},{6,7},{7,6},{8,9},{9,8},{10,11... | collective-permute-start | bytes 12582920 | tf_op jit(solution)/shard_map/ppermute | solution.py:206
  101.4 7.1 %collective-permute-done.10.oth_ref = bf16[2,1024,1024]{2,1,0:T(8,128)(2,1)} collective-permute-done((bf16[2,1024,1024]{2,1,0:T(8,128)(2,1)}, bf16[2,1024,1024]{2,1,0:T(8,128)(2,1)}, u32[]{:S(2)}, u32[]{:S(2)}) %collective-permute-start.10) | collective-permute-done | bytes 4194336 | tf_op jit(solution)/shard_map/ppermute | solution.py:206
  108.4 22.0 %all-gather.3.cloned.1.call-done = bf16[32768,128]{1,0:T(8,128)(2,1)} async-done(((bf16[1024,128]{1,0:T(8,128)(2,1)}), bf16[32768,128]{1,0:T(8,128)(2,1)}) %all-gather.3.cloned.1.call-update) | async-done | bytes 8388624 | tf_op jit(solution)/shard_map/all_gather | solution.py:212
  130.5 13.7 %project.1 = bf16[2,4,2,64,1024]{4,3,2,1,0:T(8,128)(2,1)S(1)} custom-call(s32[2]{0:T(128)S(1)} %pad_add_fusion.at, bf16[2,1024,1024]{2,1,0:T(8,128)(2,1)} %bitcast.5.own_ref, bf16[2,1024,1024]{2,1,0:T(8,128)(2,1)} %collective-permute-done.10.oth_ref, bf16[8,4,1024,128]{3,2,1,0:T(8,128)(2,1)} %bitcast.9), custom_call_target="tpu_custom_call" | custom-call | tf_op jit(solution)/shard_map/project/pallas_call | solution.py:155
  144.2 31.8 %all_to_all.5.got_ref = bf16[8,128,1024]{2,1,0:T(8,128)(2,1)S(1)} all-to-all(bf16[8,128,1024]{2,1,0:T(8,128)(2,1)S(1)} %bitcast.8), channel_id=1, replica_groups=mesh['z'=8,'xh'=2,'y'=4,'xl'=2,'c'=2] {'xh','xl','c'}, dimensions={0} | all-to-all | bytes 4194304 | tf_op jit(solution)/shard_map/all_to_all | solution.py:242
  176.0 1.8 finish.1
  (32 shorter events, 2.0 us)
Async XLA Ops:
  6.5 15.2 %copy-start.4 = (bf16[512,128]{1,0:T(8,128)(2,1)S(1)}, bf16[512,128]{1,0:T(8,128)(2,1)}, u32[]{:S(2)}) copy-start(bf16[512,128]{1,0:T(8,128)(2,1)} %param.9) | copy-start | bytes 393220
  6.5 34.9 %copy-start.2 = (s32[32768]{0:T(1024)S(1)}, s32[32768]{0:T(1024)}, u32[]{:S(2)}) copy-start(s32[32768]{0:T(1024)} %param.11) | copy-start | bytes 393220
  6.5 39.4 %copy-start = (bf16[512,1024]{1,0:T(8,128)(2,1)S(1)}, bf16[512,1024]{1,0:T(8,128)(2,1)}, u32[]{:S(2)}) copy-start(bf16[512,1024]{1,0:T(8,128)(2,1)} %q_ref.3) | copy-start | bytes 3145732
  6.5 123.9 %all-gather.3.cloned.1.call-start = ((), (), s32[]{:S(2)}) async-start(), calls=%async_computation.1 | async-start | bytes 8650752 | tf_op jit(solution)/shard_map/all_gather | solution.py:212
  6.5 9.7 %collective-permute-start.11 = (bf16[1024,128]{1,0:T(8,128)(2,1)}, bf16[1024,128]{1,0:T(8,128)(2,1)S(1)}, u32[]{:S(2)}, u32[]{:S(2)}) collective-permute-start(bf16[1024,128]{1,0:T(8,128)(2,1)} %param.12), channel_id=1, source_target_pairs={{0,0},{1,4},{2,8},{3,12},{4,1},{5,5},{6,9},{7,13},{8,2},{9,6},{10,... | collective-permute-start | bytes 786440 | tf_op jit(solution)/shard_map/ppermute | solution.py:211
  16.3 0.7 copy-start.3
  21.8 19.9 %collective-permute-start = (bf16[512,256]{1,0:T(8,128)(2,1)S(1)}, bf16[512,256]{1,0:T(8,128)(2,1)S(1)}, u32[]{:S(2)}, u32[]{:S(2)}) collective-permute-start(bf16[512,256]{1,0:T(8,128)(2,1)S(1)} %pad_maximum_fusion.2.kv0), channel_id=1, source_target_pairs={{0,4},{4,8},{8,12},{12,16},{16,20},{20,24},{24,28},{28,32},{32,36}... | collective-permute-start | bytes 786440 | tf_op jit(solution)/shard_map/ppermute | solution.py:32
  23.1 18.6 %collective-permute-start.1 = (bf16[512,256]{1,0:T(8,128)(2,1)S(1)}, bf16[512,256]{1,0:T(8,128)(2,1)S(1)}, u32[]{:S(2)}, u32[]{:S(2)}) collective-permute-start(bf16[512,256]{1,0:T(8,128)(2,1)S(1)} %pad_maximum_fusion.2.kv0), channel_id=1, source_target_pairs={{0,8},{4,12},{8,16},{12,20},{16,24},{20,28},{24,32},{28,36},{32,40... | collective-permute-start | bytes 786440 | tf_op jit(solution)/shard_map/ppermute | solution.py:32
  33.4 12.4 %collective-permute-start.2 = (bf16[512,256]{1,0:T(8,128)(2,1)S(1)}, bf16[512,256]{1,0:T(8,128)(2,1)S(1)}, u32[]{:S(2)}, u32[]{:S(2)}) collective-permute-start(bf16[512,256]{1,0:T(8,128)(2,1)S(1)} %pad_maximum_fusion.2.kv0), channel_id=1, source_target_pairs={{0,12},{4,16},{8,20},{12,24},{16,28},{20,32},{24,36},{28,40},{32,4... | collective-permute-start | bytes 786440 | tf_op jit(solution)/shard_map/ppermute | solution.py:32
  37.9 7.9 %collective-permute-start.3 = (bf16[512,256]{1,0:T(8,128)(2,1)S(1)}, bf16[512,256]{1,0:T(8,128)(2,1)S(1)}, u32[]{:S(2)}, u32[]{:S(2)}) collective-permute-start(bf16[512,256]{1,0:T(8,128)(2,1)S(1)} %pad_maximum_fusion.2.kv0), channel_id=1, source_target_pairs={{0,16},{4,20},{8,24},{12,28},{16,32},{20,36},{24,40},{28,44},{32,4... | collective-permute-start | bytes 786440 | tf_op jit(solution)/shard_map/ppermute | solution.py:32
  48.7 18.7 %collective-permute-start.4 = (bf16[256,1024]{1,0:T(8,128)(2,1)S(1)}, bf16[256,1024]{1,0:T(8,128)(2,1)S(1)}, u32[]{:S(2)}, u32[]{:S(2)}) collective-permute-start(bf16[256,1024]{1,0:T(8,128)(2,1)S(1)} %shard_map.73), channel_id=1, source_target_pairs={{0,18},{2,16},{16,2},{18,0},{1,19},{3,17},{17,3},{19,1},{4,22},{6,... | collective-permute-start | bytes 1572872 | tf_op jit(solution)/shard_map/ppermute | solution.py:195
  60.0 11.1 %collective-permute-start.6 = (bf16[256,1024]{1,0:T(8,128)(2,1)S(1)}, bf16[256,1024]{1,0:T(8,128)(2,1)S(1)}, u32[]{:S(2)}, u32[]{:S(2)}) collective-permute-start(bf16[256,1024]{1,0:T(8,128)(2,1)S(1)} %shard_map.74), channel_id=1, source_target_pairs={{0,2},{2,0},{16,18},{18,16},{1,3},{3,1},{17,19},{19,17},{4,6},{6,4... | collective-permute-start | bytes 1572872 | tf_op jit(solution)/shard_map/ppermute | solution.py:195
  67.4 14.9 %collective-permute-start.5 = (bf16[256,1024]{1,0:T(8,128)(2,1)S(1)}, bf16[256,1024]{1,0:T(8,128)(2,1)S(1)}, u32[]{:S(2)}, u32[]{:S(2)}) collective-permute-start(bf16[256,1024]{1,0:T(8,128)(2,1)S(1)} %collective-permute-done.4), channel_id=1, source_target_pairs={{0,2},{2,0},{16,18},{18,16},{1,3},{3,1},{17,19},{19,17},{4,6},{6,4... | collective-permute-start | bytes 1572872 | tf_op jit(solution)/shard_map/ppermute | solution.py:195
  71.1 12.1 %collective-permute-start.7 = (bf16[256,1024]{1,0:T(8,128)(2,1)S(1)}, bf16[256,1024]{1,0:T(8,128)(2,1)S(1)}, u32[]{:S(2)}, u32[]{:S(2)}) collective-permute-start(bf16[256,1024]{1,0:T(8,128)(2,1)S(1)} %collective-permute-done.6), channel_id=1, source_target_pairs={{0,18},{2,16},{16,2},{18,0},{1,19},{3,17},{17,3},{19,1},{4,22},{6,... | collective-permute-start | bytes 1572872 | tf_op jit(solution)/shard_map/ppermute | solution.py:195
  76.4 17.3 %collective-permute-start.8 = (bf16[256,1024]{1,0:T(8,128)(2,1)S(1)}, bf16[256,1024]{1,0:T(8,128)(2,1)S(1)}, u32[]{:S(2)}, u32[]{:S(2)}) collective-permute-start(bf16[256,1024]{1,0:T(8,128)(2,1)S(1)} %shard_map.73), channel_id=1, source_target_pairs={{0,2},{2,0},{16,18},{18,16},{1,3},{3,1},{17,19},{19,17},{4,6},{6,4... | collective-permute-start | bytes 1572872 | tf_op jit(solution)/shard_map/ppermute | solution.py:195
  76.4 19.8 %collective-permute-start.9 = (bf16[256,1024]{1,0:T(8,128)(2,1)S(1)}, bf16[256,1024]{1,0:T(8,128)(2,1)S(1)}, u32[]{:S(2)}, u32[]{:S(2)}) collective-permute-start(bf16[256,1024]{1,0:T(8,128)(2,1)S(1)} %shard_map.74), channel_id=1, source_target_pairs={{0,18},{2,16},{16,2},{18,0},{1,19},{3,17},{17,3},{19,1},{4,22},{6,... | collective-permute-start | bytes 1572872 | tf_op jit(solution)/shard_map/ppermute | solution.py:195
  97.0 11.5 %collective-permute-start.10 = (bf16[2,1024,1024]{2,1,0:T(8,128)(2,1)}, bf16[2,1024,1024]{2,1,0:T(8,128)(2,1)}, u32[]{:S(2)}, u32[]{:S(2)}) collective-permute-start(bf16[2,1024,1024]{2,1,0:T(8,128)(2,1)} %bitcast.5.own_ref), channel_id=1, source_target_pairs={{0,1},{1,0},{2,3},{3,2},{4,5},{5,4},{6,7},{7,6},{8,9},{9,8},{10,11... | collective-permute-start | bytes 12582920 | tf_op jit(solution)/shard_map/ppermute | solution.py:206
  144.2 31.8 %copy-start.1 = (bf16[128,8192]{1,0:T(8,128)(2,1)S(1)}, bf16[128,8192]{1,0:T(8,128)(2,1)}, u32[]{:S(2)}) copy-start(bf16[128,8192]{1,0:T(8,128)(2,1)} %res_ref.1) | copy-start | bytes 6291460
Sparse Core Ops, SparseCore 0:
  17.1 113.3 all-gather.2
